TPU v7x, 32 devices: a whole 2x2x4 slice. The times are simulated.
32 devices in a mesh: seq: 2 (over x), row: 4 (over y, core), col: 4 (over z).
Axes of the slice: x: 2, y: 2, z: 4, core: 2. Of those that a mesh axis runs over, the one named last changes fastest.
Arguments:
- activations: bfloat16 [2, 64, 8192], P(None, 'row', 'seq'), may hold values from -6 to 6
- gradients: bfloat16 [2, 64, 8192], P(None, 'col', 'seq'), may hold values from -6 to 6
- basis_in: bfloat16 [8192, 4096], P('seq', 'col'), may hold values from -0.0625 to 0.0625
- basis_out: bfloat16 [8192, 4096], P('seq', 'row'), may hold values from -0.0625 to 0.0625
- lengths: int32 [2], replicated, may hold values from 16 to 64
Outputs:
- corrections: float32 [4096, 4096], P(('row', 'seq'), 'col')
All inputs are finite; a program needn't handle non-finite values.
Results may differ from a plain program's by a relative error of at most 0.0023.
Values may be sent and summed in bfloat16 or wider, within the bound.
No kernel may reach another device: no remote copies, remote signals or barrier semaphores. Data moves between devices by JAX's collectives and lax.ppermute only.
A program may use at most 64 MiB of HBM per device.

v0:
```python
import jax
import jax.numpy as jnp
from jax import lax
from jax.sharding import PartitionSpec as P


def turned_terms(tokens, basis):
    return jnp.einsum("ntf,fk->ntk", tokens, basis, preferred_element_type=jnp.float32)


def local(activations, gradients, basis_in, basis_out, lengths):
    seq_count = lax.axis_size("seq")
    seq_index = lax.axis_index("seq")
    length = lengths[seq_index]
    summed_in = lax.psum_scatter(
        turned_terms(activations, basis_in), "seq", scatter_dimension=0, tiled=True
    )
    turned_in = summed_in[0].astype(jnp.bfloat16)
    summed_out = lax.psum_scatter(
        turned_terms(gradients, basis_out), "seq", scatter_dimension=0, tiled=True
    )
    turned_out = summed_out[0].astype(jnp.bfloat16)
    every_in = lax.all_gather(turned_in, "row", axis=0, tiled=True)
    every_out = lax.all_gather(turned_out, "col", axis=0, tiled=True)
    slot_total = every_in.shape[0]
    slots = jnp.arange(slot_total)
    contract = (((0,), (0,)), ((), ()))
    kept = jnp.where((slots < length)[:, None], every_out, jnp.zeros((), jnp.bfloat16))
    product_tile = lax.dot_general(kept, every_in, contract, preferred_element_type=jnp.float32)
    squared = product_tile * product_tile / (seq_count * slot_total)
    return lax.psum_scatter(squared, "seq", scatter_dimension=0, tiled=True)


def solution(mesh):
    return jax.shard_map(
        local,
        mesh=mesh,
        in_specs=(
            P(None, "row", "seq"),
            P(None, "col", "seq"),
            P("seq", "col"),
            P("seq", "row"),
            P(),
        ),
        out_specs=P(("row", "seq"), "col"),
        check_vma=False,
    )
```

profile of v0, /device:TPU:0, one launch (start us, length us, event | category | flops | bytes accessed | tf_op | source)
XLA Modules:
  0.0 117.2 jit_solution(11242291318039714321)
XLA Ops:
  6.5 0.0 copy-start
  6.5 0.0 copy-start.1
  6.5 0.0 reduce-scatter.6.cloned.1.call-start
  6.5 0.9 copy-done
  7.5 5.6 %fusion = f32[2,16,1024]{2,1,0:T(8,128)} fusion(bf16[2,16,4096]{2,1,0:T(8,128)(2,1)S(1)} %copy-done, bf16[4096,1024]{1,0:T(8,128)(2,1)} %param.7), kind=kOutput, calls=%fused_computation | convolution fusion | flops 268435456 | bytes 8781824 | tf_op jit(solution)/shard_map/ntf,fk->ntk/dot_general | solution.py:8
  13.1 0.0 copy-start.2
  13.1 0.0 reduce-scatter.6.cloned.1.call-update
  13.1 0.0 reduce-scatter.4.cloned.1.call-start
  13.1 0.0 copy-done.1
  13.2 5.6 %fusion.2 = f32[2,16,1024]{2,1,0:T(8,128)} fusion(bf16[2,16,4096]{2,1,0:T(8,128)(2,1)S(1)} %copy-done.1, bf16[4096,1024]{1,0:T(8,128)(2,1)} %param.8), kind=kOutput, calls=%fused_computation.2 | convolution fusion | flops 268435456 | bytes 8781824 | tf_op jit(solution)/shard_map/ntf,fk->ntk/dot_general | solution.py:8
  18.7 0.0 reduce-scatter.4.cloned.1.call-update
  18.8 0.0 reduce-scatter.8.cloned.1.call-start
  18.8 0.0 copy-done.2
  18.8 0.7 dynamic_slice.3
  19.5 0.7 iota_compare_fusion
  20.2 6.1 %reduce-scatter.6.cloned.1.call-done = f32[1,16,1024]{2,1,0:T(8,128)} async-done(((f32[2,16,1024]{2,1,0:T(8,128)}), f32[1,16,1024]{2,1,0:T(8,128)}) %reduce-scatter.6.cloned.1.call-update) | async-done | bytes 65552 | tf_op jit(solution)/shard_map/reduce_scatter | solution.py:15
  26.3 0.8 convert_element_type.14
  27.2 5.4 %all-gather.1 = bf16[1,64,1024]{2,1,0:T(8,128)(2,1)S(1)} all-gather(bf16[1,16,1024]{2,1,0:T(8,128)(2,1)S(1)} %convert_element_type.14), channel_id=3, replica_groups=mesh['seq'=2,'row'=4,'col'=4] {'row'}, dimensions={1}, use_global_device_ids=true | all-gather | bytes 163840 | tf_op jit(solution)/shard_map/all_gather | solution.py:23
  32.6 6.4 %reduce-scatter.4.cloned.1.call-done = f32[1,16,1024]{2,1,0:T(8,128)} async-done(((f32[2,16,1024]{2,1,0:T(8,128)}), f32[1,16,1024]{2,1,0:T(8,128)}) %reduce-scatter.4.cloned.1.call-update) | async-done | bytes 65552 | tf_op jit(solution)/shard_map/reduce_scatter | solution.py:19
  38.9 0.8 convert_element_type.12
  39.8 13.4 %all-gather = bf16[1,64,1024]{2,1,0:T(8,128)(2,1)S(1)} all-gather(bf16[1,16,1024]{2,1,0:T(8,128)(2,1)S(1)} %convert_element_type.12), channel_id=2, replica_groups=mesh['seq'=2,'row'=4,'col'=4] {'col'}, dimensions={1}, use_global_device_ids=true | all-gather | bytes 163840 | tf_op jit(solution)/shard_map/all_gather | solution.py:24
  53.2 2.8 %multiply_multiply_fusion = f32[1024,1024]{1,0:T(8,128)} fusion(bf16[1,64,1024]{2,1,0:T(8,128)(2,1)S(1)} %all-gather.1, bf16[1,64,1024]{2,1,0:T(8,128)(2,1)S(1)} %all-gather, pred[64]{0:T(512)(128)(4,1)S(1)} %iota_compare_fusion), kind=kOutput, calls=%fused_computation.4 | convolution fusion | flops 136380416 | bytes 4456512 | tf_op jit(solution)/shard_map/dot_general | solution.py:29
  56.0 0.0 reduce-scatter.8.cloned.1.call-update
  56.0 54.7 %reduce-scatter.8.cloned.1.call-done = f32[512,1024]{1,0:T(8,128)} async-done(((f32[1024,1024]{1,0:T(8,128)}), f32[512,1024]{1,0:T(8,128)}) %reduce-scatter.8.cloned.1.call-update) | async-done | bytes 2097168 | tf_op jit(solution)/shard_map/reduce_scatter | solution.py:31
Async XLA Ops:
  6.5 1.0 copy-start
  6.5 6.6 %copy-start.1 = (bf16[2,16,4096]{2,1,0:T(8,128)(2,1)S(1)}, bf16[2,16,4096]{2,1,0:T(8,128)(2,1)}, u32[]{:S(2)}) copy-start(bf16[2,16,4096]{2,1,0:T(8,128)(2,1)} %param.6) | copy-start | bytes 786436
  6.5 19.8 %reduce-scatter.6.cloned.1.call-start = ((), (), s32[]{:S(2)}) async-start(), calls=%async_computation.4 | async-start | bytes 196608 | tf_op jit(solution)/shard_map/reduce_scatter | solution.py:15
  13.1 5.7 %copy-start.2 = (s32[2]{0:T(128)S(1)}, s32[2]{0:T(128)}, u32[]{:S(2)}) copy-start(s32[2]{0:T(128)} %param.9) | copy-start | bytes 28
  13.1 25.8 %reduce-scatter.4.cloned.1.call-start = ((), (), s32[]{:S(2)}) async-start(), calls=%async_computation.3 | async-start | bytes 196608 | tf_op jit(solution)/shard_map/reduce_scatter | solution.py:19
  18.8 92.0 %reduce-scatter.8.cloned.1.call-start = ((), (), s32[]{:S(2)}) async-start(), calls=%async_computation.5 | async-start | bytes 6291456 | tf_op jit(solution)/shard_map/reduce_scatter | solution.py:31
Sparse Core Ops, SparseCore 0:
  13.2 13.0 reduce-scatter.5
  28.5 10.3 reduce-scatter.3
  56.1 54.5 reduce-scatter.7
where the time goes:
time: 118 us; the launch traced here: 117 us
  waiting for transfers between devices  67.3 us (57%)
  blocking collectives  18.8 us (16%)
  matrix products  13.9 us (12%)
  between operations  13.1 us (11%)
  other arithmetic  2.38 us (2%)
  local copies, waits for them, and re-layouts  1.62 us (1%)
    reduce_scatter x1, waiting for transfers between devices, local(): return lax.psum_scatter(squared, 'seq', scatter_dimension=0, tiled=True)  54.7 us
    all_gather x1, blocking collectives, local(): every_out = lax.all_gather(turned_out, 'col', axis=0, tiled=True)  13.4 us
    dot_general x2, matrix products, turned_terms(): jnp.einsum('ntf,fk->ntk', tokens, basis, preferred_element_type=jnp.float32)  11.2 us
    reduce_scatter x1, waiting for transfers between devices, local(): lax.psum_scatter(turned_terms(gradients, basis_out), 'seq', scatter_dimen...  6.36 us
    reduce_scatter x1, waiting for transfers between devices, local(): lax.psum_scatter(turned_terms(activations, basis_in), 'seq', scatter_dime...  6.15 us
    all_gather x1, blocking collectives, local(): every_in = lax.all_gather(turned_in, 'row', axis=0, tiled=True)  5.4 us
    dot_general x1, matrix products, local(): lax.dot_general(kept, every_in, contract, preferred_element_type=jnp.floa...  2.75 us
  transfers between devices with their start and end apart: 3, of which 3 were waited for; matrix products, arithmetic and copies ran while one was open for 7% of the time, Pallas kernels for 0%

commit v1 on v0

--- a/solution.py
+++ b/solution.py
@@ -2,6 +2,19 @@
 import jax.numpy as jnp
 from jax import lax
 from jax.sharding import PartitionSpec as P
+from jax.lax import axis_index, axis_size, ppermute
+
+
+def sector_watch(inp):
+    n_dev_all = axis_size("col")
+    f_next = list(map(lambda dev_i: (dev_i - 1, dev_i), range(1, n_dev_all))) + [(n_dev_all - 1, 0)]
+    f_now = inp
+    panels = [f_now]
+    for _ in tuple(range(n_dev_all - 1)):
+        f_now = ppermute(f_now, "col", f_next)
+        panels += [f_now]
+    fresh = jnp.concatenate([*reversed(panels)], axis=0)
+    return jnp.roll(fresh, shift=(axis_index("col") + 1) * f_now.shape[0], axis=0)
 
 
 def turned_terms(tokens, basis):
@@ -21,7 +34,7 @@
     )
     turned_out = summed_out[0].astype(jnp.bfloat16)
     every_in = lax.all_gather(turned_in, "row", axis=0, tiled=True)
-    every_out = lax.all_gather(turned_out, "col", axis=0, tiled=True)
+    every_out = sector_watch(turned_out)
     slot_total = every_in.shape[0]
     slots = jnp.arange(slot_total)
     contract = (((0,), (0,)), ((), ()))

time: 118 us -> 112 us (0.949)
  blocking collectives: 18.8 us -> 5.4 us
  starting transfers between devices: 0.09 us -> 3.05 us
  waiting for transfers between devices: 67.3 us -> 70.1 us
  other arithmetic: 2.38 us -> 4.07 us
    all_gather x1 -> x0, blocking collectives: 13.4 us -> none  [local(): every_out = lax.all_gather(turned_out, 'col', axis=0, tiled=True)]
    ppermute x0 -> x3, waiting for transfers between devices: none -> 3.57 us  [sector_watch(): f_now = ppermute(f_now, 'col', f_next)]
    ppermute x0 -> x3, starting transfers between devices: none -> 2.97 us  [sector_watch(): f_now = ppermute(f_now, 'col', f_next)]
  transfers between devices with their start and end apart: 3 -> 6, of which waited for: 3 -> 4; matrix products, arithmetic and copies ran while one was open for 7% -> 8% of each run, Pallas kernels for 0% -> 0%
where the time goes in v1:
time: 112 us; the launch traced here: 111 us
  waiting for transfers between devices  70.1 us (63%)
  matrix products  13.9 us (12%)
  between operations  13.2 us (12%)
  blocking collectives  5.4 us (5%)
  other arithmetic  4.07 us (4%)
  starting transfers between devices  3.05 us (3%)
  local copies, waits for them, and re-layouts  1.64 us (1%)
    reduce_scatter x1, waiting for transfers between devices, local(): return lax.psum_scatter(squared, 'seq', scatter_dimension=0, tiled=True)  53.6 us
    dot_general x2, matrix products, turned_terms(): jnp.einsum('ntf,fk->ntk', tokens, basis, preferred_element_type=jnp.float32)  11.2 us
    reduce_scatter x1, waiting for transfers between devices, local(): lax.psum_scatter(turned_terms(gradients, basis_out), 'seq', scatter_dimen...  7.52 us
    all_gather x1, blocking collectives, local(): every_in = lax.all_gather(turned_in, 'row', axis=0, tiled=True)  5.4 us
    reduce_scatter x1, waiting for transfers between devices, local(): lax.psum_scatter(turned_terms(activations, basis_in), 'seq', scatter_dime...  5.32 us
    ppermute x3, waiting for transfers between devices, sector_watch(): f_now = ppermute(f_now, 'col', f_next)  3.57 us
    ppermute x3, starting transfers between devices, sector_watch(): f_now = ppermute(f_now, 'col', f_next)  2.97 us
    dot_general x1, matrix products, local(): lax.dot_general(kept, every_in, contract, preferred_element_type=jnp.floa...  2.75 us
  transfers between devices with their start and end apart: 6, of which 4 were waited for; matrix products, arithmetic and copies ran while one was open for 8% of the time, Pallas kernels for 0%

profile of v1, /device:TPU:0, one launch (start us, length us, event | category | flops | bytes accessed | tf_op | source)
XLA Modules:
  0.0 111.3 jit_solution(13100850115560379669)
XLA Ops:
  6.5 0.0 copy-start
  6.5 0.0 copy-start.1
  6.5 0.0 reduce-scatter.4.cloned.1.call-start
  6.5 0.9 copy-done
  7.5 5.6 %fusion.2 = f32[2,16,1024]{2,1,0:T(8,128)} fusion(bf16[2,16,4096]{2,1,0:T(8,128)(2,1)S(1)} %copy-done, bf16[4096,1024]{1,0:T(8,128)(2,1)} %param.8), kind=kOutput, calls=%fused_computation.2 | convolution fusion | flops 268435456 | bytes 8781824 | tf_op jit(solution)/shard_map/ntf,fk->ntk/dot_general | solution.py:21
  13.1 0.0 copy-start.2
  13.1 0.0 reduce-scatter.4.cloned.1.call-update
  13.1 0.0 reduce-scatter.6.cloned.1.call-start
  13.1 0.0 copy-done.1
  13.1 5.6 %fusion = f32[2,16,1024]{2,1,0:T(8,128)} fusion(bf16[2,16,4096]{2,1,0:T(8,128)(2,1)S(1)} %copy-done.1, bf16[4096,1024]{1,0:T(8,128)(2,1)} %param.7), kind=kOutput, calls=%fused_computation | convolution fusion | flops 268435456 | bytes 8781824 | tf_op jit(solution)/shard_map/ntf,fk->ntk/dot_general | solution.py:21
  18.7 0.0 reduce-scatter.6.cloned.1.call-update
  18.8 0.0 reduce-scatter.8.cloned.1.call-start
  18.8 7.5 %reduce-scatter.4.cloned.1.call-done = f32[1,16,1024]{2,1,0:T(8,128)} async-done(((f32[2,16,1024]{2,1,0:T(8,128)}), f32[1,16,1024]{2,1,0:T(8,128)}) %reduce-scatter.4.cloned.1.call-update) | async-done | bytes 65552 | tf_op jit(solution)/shard_map/reduce_scatter | solution.py:32
  26.3 0.8 convert_bitcast_fusion
  27.2 1.5 %collective-permute-start = (bf16[16,1024]{1,0:T(8,128)(2,1)S(1)}, bf16[16,1024]{1,0:T(8,128)(2,1)S(1)}, u32[]{:S(2)}, u32[]{:S(2)}) collective-permute-start(bf16[16,1024]{1,0:T(8,128)(2,1)S(1)} %convert_bitcast_fusion), channel_id=1, source_target_pairs={{0,1},{1,2},{2,3},{3,0},{4,5},{5,6},{6,7},{7,4},{8,9},{9,10},{10,1... | collective-permute-start | bytes 98312 | tf_op jit(solution)/shard_map/ppermute | solution.py:14
  28.7 0.0 copy-done.2
  28.7 0.7 dynamic_slice.7
  29.3 3.6 %collective-permute-done = bf16[16,1024]{1,0:T(8,128)(2,1)S(1)} collective-permute-done((bf16[16,1024]{1,0:T(8,128)(2,1)S(1)}, bf16[16,1024]{1,0:T(8,128)(2,1)S(1)}, u32[]{:S(2)}, u32[]{:S(2)}) %collective-permute-start) | collective-permute-done | bytes 32800 | tf_op jit(solution)/shard_map/ppermute | solution.py:14
  32.9 0.0 collective-permute-start.1
  32.9 0.7 iota_compare_fusion
  33.6 5.3 %reduce-scatter.6.cloned.1.call-done = f32[1,16,1024]{2,1,0:T(8,128)} async-done(((f32[2,16,1024]{2,1,0:T(8,128)}), f32[1,16,1024]{2,1,0:T(8,128)}) %reduce-scatter.6.cloned.1.call-update) | async-done | bytes 65552 | tf_op jit(solution)/shard_map/reduce_scatter | solution.py:28
  38.9 0.8 convert_element_type.14
  39.8 0.0 collective-permute-done.1
  39.8 1.5 %collective-permute-start.2 = (bf16[16,1024]{1,0:T(8,128)(2,1)S(1)}, bf16[16,1024]{1,0:T(8,128)(2,1)S(1)}, u32[]{:S(2)}, u32[]{:S(2)}) collective-permute-start(bf16[16,1024]{1,0:T(8,128)(2,1)S(1)} %collective-permute-done.1), channel_id=1, source_target_pairs={{0,1},{1,2},{2,3},{3,0},{4,5},{5,6},{6,7},{7,4},{8,9},{9,10},{10,1... | collective-permute-start | bytes 98312 | tf_op jit(solution)/shard_map/ppermute | solution.py:14
  41.3 5.4 %all-gather = bf16[1,64,1024]{2,1,0:T(8,128)(2,1)S(1)} all-gather(bf16[1,16,1024]{2,1,0:T(8,128)(2,1)S(1)} %convert_element_type.14), channel_id=2, replica_groups=mesh['seq'=2,'row'=4,'col'=4] {'row'}, dimensions={1}, use_global_device_ids=true | all-gather | bytes 163840 | tf_op jit(solution)/shard_map/all_gather | solution.py:36
  46.7 0.0 collective-permute-done.2
  46.7 0.8 constant_dynamic-update-slice_fusion.4
  47.6 0.8 constant_dynamic-update-slice_fusion
  48.4 2.7 %multiply_multiply_fusion = f32[1024,1024]{1,0:T(8,128)} fusion(bf16[1,64,1024]{2,1,0:T(8,128)(2,1)S(1)} %all-gather, bf16[128,1024]{1,0:T(8,128)(2,1)S(1)} %constant_dynamic-update-slice_fusion, s32[]{:T(128)S(6)} %select_n.22, pred[64]{0:T(512)(128)(4,1)S(1)} %iota_compare_fusion), kind=kOutput, calls=%fused_computation.4 | convolution fusion | flops 136380416 | bytes 4456964 | tf_op jit(solution)/shard_map/dot_general | solution.py:42
  51.1 0.0 reduce-scatter.8.cloned.1.call-update
  51.2 53.6 %reduce-scatter.8.cloned.1.call-done = f32[512,1024]{1,0:T(8,128)} async-done(((f32[1024,1024]{1,0:T(8,128)}), f32[512,1024]{1,0:T(8,128)}) %reduce-scatter.8.cloned.1.call-update) | async-done | bytes 2097168 | tf_op jit(solution)/shard_map/reduce_scatter | solution.py:44
  (6 shorter events, 0.0 us)
Async XLA Ops:
  6.5 1.0 copy-start
  6.5 6.6 %copy-start.1 = (bf16[2,16,4096]{2,1,0:T(8,128)(2,1)S(1)}, bf16[2,16,4096]{2,1,0:T(8,128)(2,1)}, u32[]{:S(2)}) copy-start(bf16[2,16,4096]{2,1,0:T(8,128)(2,1)} %param.5) | copy-start | bytes 786436
  6.5 19.8 %reduce-scatter.4.cloned.1.call-start = ((), (), s32[]{:S(2)}) async-start(), calls=%async_computation.3 | async-start | bytes 196608 | tf_op jit(solution)/shard_map/reduce_scatter | solution.py:32
  13.1 15.6 %copy-start.2 = (s32[2]{0:T(128)S(1)}, s32[2]{0:T(128)}, u32[]{:S(2)}) copy-start(s32[2]{0:T(128)} %param.9) | copy-start | bytes 28
  13.1 25.8 %reduce-scatter.6.cloned.1.call-start = ((), (), s32[]{:S(2)}) async-start(), calls=%async_computation.4 | async-start | bytes 196608 | tf_op jit(solution)/shard_map/reduce_scatter | solution.py:28
  18.8 86.0 %reduce-scatter.8.cloned.1.call-start = ((), (), s32[]{:S(2)}) async-start(), calls=%async_computation.5 | async-start | bytes 6291456 | tf_op jit(solution)/shard_map/reduce_scatter | solution.py:44
  27.2 5.7 %collective-permute-start = (bf16[16,1024]{1,0:T(8,128)(2,1)S(1)}, bf16[16,1024]{1,0:T(8,128)(2,1)S(1)}, u32[]{:S(2)}, u32[]{:S(2)}) collective-permute-start(bf16[16,1024]{1,0:T(8,128)(2,1)S(1)} %convert_bitcast_fusion), channel_id=1, source_target_pairs={{0,1},{1,2},{2,3},{3,0},{4,5},{5,6},{6,7},{7,4},{8,9},{9,10},{10,1... | collective-permute-start | bytes 98312 | tf_op jit(solution)/shard_map/ppermute | solution.py:14
  32.9 6.9 %collective-permute-start.1 = (bf16[16,1024]{1,0:T(8,128)(2,1)S(1)}, bf16[16,1024]{1,0:T(8,128)(2,1)S(1)}, u32[]{:S(2)}, u32[]{:S(2)}) collective-permute-start(bf16[16,1024]{1,0:T(8,128)(2,1)S(1)} %collective-permute-done), channel_id=1, source_target_pairs={{0,1},{1,2},{2,3},{3,0},{4,5},{5,6},{6,7},{7,4},{8,9},{9,10},{10,1... | collective-permute-start | bytes 98312 | tf_op jit(solution)/shard_map/ppermute | solution.py:14
  39.8 6.9 %collective-permute-start.2 = (bf16[16,1024]{1,0:T(8,128)(2,1)S(1)}, bf16[16,1024]{1,0:T(8,128)(2,1)S(1)}, u32[]{:S(2)}, u32[]{:S(2)}) collective-permute-start(bf16[16,1024]{1,0:T(8,128)(2,1)S(1)} %collective-permute-done.1), channel_id=1, source_target_pairs={{0,1},{1,2},{2,3},{3,0},{4,5},{5,6},{6,7},{7,4},{8,9},{9,10},{10,1... | collective-permute-start | bytes 98312 | tf_op jit(solution)/shard_map/ppermute | solution.py:14
Sparse Core Ops, SparseCore 0:
  13.2 13.0 reduce-scatter.3
  28.5 10.3 reduce-scatter.5
  51.3 53.4 reduce-scatter.7
